TPU v7x, 512 devices: a whole 4x4x16 slice. The times are simulated.
512 devices in a mesh: ka: 128 (over y, x_hi, z), col: 4 (over x_lo, core).
Axes of the slice: x: 4 (x_hi: 2, x_lo: 2; x = x_hi * 2 + x_lo), y: 4, z: 16, core: 2. Of those that a mesh axis runs over, the one named last changes fastest.
Arguments:
- amps: bfloat16 [256, 256, 192], P('ka', 'col'), may hold values from -6 to 6
- isdf_coeffs: bfloat16 [256, 2048, 256], P('ka', 'col'), may hold values from -0.375 to 0.375
- w_screen: bfloat16 [16, 2048, 2048], P(None, 'ka', 'col'), as said below
- energies: float32 [256, 256], P('ka', 'col'), may hold values from 0.5 to 3
- qsel: int32 [2], replicated, may hold values from 0 to 15
- partner: int32 [2, 256], replicated, may hold values from 0 to 255, each once within a row
Outputs:
- applied: float32 [256, 256, 192], P('ka', 'col')
Inputs may be any that keep to these rules, and one draw needn't show every extreme that they name: Each row of partner is a permutation of the 256 k points. `w_screen`: each of the 16 matrices is symmetric.
All inputs are finite; a program needn't handle non-finite values.
Results may differ from a plain program's by a relative error of at most 0.013.
Values may be sent and summed in bfloat16 or wider, within the bound.
No kernel may reach another device: no remote copies, remote signals or barrier semaphores. Data moves between devices by JAX's collectives and lax.ppermute only.
A program may use at most 64 MiB of HBM per device.

v0:
```python
import jax
import jax.numpy as jnp
from jax import lax
from jax.sharding import Mesh
from jax.sharding import PartitionSpec as P

KA = ("ka_0", "ka_1", "ka_2")


def laid_out(pieces, dim):
    lengths = list(pieces.shape[1:])
    lengths[dim] *= pieces.shape[0]
    return jnp.moveaxis(pieces, 0, dim).reshape(lengths)


def gather_in_order(array, axes, order):
    pieces = array[None]
    for k in order:
        pieces = lax.all_gather(pieces, axes[k], axis=0, tiled=True)
    carried = [lax.axis_size(axes[k]) for k in reversed(order)]
    pieces = pieces.reshape(*carried, *array.shape)
    turned = sorted(range(len(order)), key=lambda place: order[len(order) - 1 - place])
    return pieces.transpose(*turned, *range(len(order), pieces.ndim)).reshape(-1, *array.shape)


def gather_axes(array, axes, order, dim):
    return laid_out(gather_in_order(array, axes, order), dim)


def sent_to_all(array, axis):
    length = lax.axis_size(axis)
    return lax.all_to_all(
        jnp.broadcast_to(array[None], (length, *array.shape)), axis, 0, 0, tiled=True
    )


def collect(array, axis, dim):
    pieces = sent_to_all(array, axis)
    return laid_out(pieces, dim)


def split_up(array, dim, length):
    before, after = (array.shape[:dim], array.shape[dim + 1 :])
    return jnp.moveaxis(array.reshape(*before, length, -1, *after), dim, 0)


def sent_and_summed(array, axis, dim):
    pieces = split_up(array, dim, lax.axis_size(axis))
    arrived = lax.all_to_all(pieces, axis, split_axis=0, concat_axis=0, tiled=True)
    return arrived.astype(jnp.float32).sum(axis=0)


def body(amps, isdf_coeffs, w_screen, energies, qsel, partner):
    k_local = amps.shape[0]
    vectors = amps.shape[2]
    offset_base = lax.axis_index(KA) * k_local
    owned = offset_base + jnp.arange(k_local, dtype=jnp.int32)
    wanted = jnp.take(partner, owned, axis=1).reshape(-1)
    everyone = gather_axes(amps, KA, (1, 0, 2), 0)
    picked = jnp.take(everyone, wanted, axis=0)
    partners = collect(picked, "col", 1)
    partners = partners.reshape(2, k_local, partners.shape[1], vectors)
    densities = jnp.einsum(
        "kms,qkse->qmke", isdf_coeffs, partners, preferred_element_type=jnp.float32
    )
    width = densities.shape[1]
    densities = densities.astype(jnp.bfloat16).reshape(2, width, k_local * vectors)
    slabs = jnp.take(w_screen, qsel, axis=0)
    partials = jnp.einsum(
        "qrm,qmx->qrx",
        lax.all_gather(slabs, KA, axis=1, tiled=True),
        densities,
        preferred_element_type=jnp.float32,
    )
    screened = sent_and_summed(partials.astype(jnp.bfloat16), "col", 1)
    screened = screened.astype(jnp.bfloat16).reshape(2, width, k_local, vectors)
    projected = jnp.einsum(
        "kms,qmke->kse", isdf_coeffs, screened, preferred_element_type=jnp.float32
    )
    summed = sent_and_summed(projected.astype(jnp.bfloat16), "col", 1)
    return summed + energies[:, :, None] * amps.astype(jnp.float32)


def solution(mesh):
    torus = Mesh(mesh.devices.reshape(4, 2, 16, mesh.shape["col"]), ("ka_0", "ka_1", "ka_2", "col"))
    placed = (P(KA, "col", None), P(KA, "col", None), P(None, KA, "col"), P(KA, "col"), P(), P())
    return jax.shard_map(
        body, mesh=torus, in_specs=placed, out_specs=P(KA, "col", None), check_vma=False
    )
```

profile of v0, /device:TPU:1, one launch (start us, length us, event | category | flops | bytes accessed | tf_op | source)
XLA Modules:
  0.0 428.2 jit_solution(16825926341223506665)
XLA Ops:
  6.5 6.3 %all-gather = bf16[4,64,192]{2,1,0:T(8,128)(2,1)S(1)} all-gather(bf16[2,64,192]{2,1,0:T(8,128)(2,1)} %param.6), channel_id=2, replica_groups=mesh['ka_0'=4,'ka_1'=2,'ka_2'=16,'col'=4] {'ka_1'}, dimensions={0}, use_global_device_ids=true | all-gather | bytes 147456 | tf_op jit(solution)/shard_map/all_gather | solution.py:19
  12.8 11.5 %all_gather.14 = bf16[8,2,64,192]{3,2,1,0:T(8,128)(2,1)} all-gather(bf16[2,2,64,192]{3,2,1,0:T(8,128)(2,1)S(1)} %bitcast.44), channel_id=1, replica_groups=mesh['ka_0'=4,'ka_1'=2,'ka_2'=16,'col'=4] {'ka_0'}, dimensions={0}, use_global_device_ids=true | all-gather | bytes 491520 | tf_op jit(solution)/shard_map/all_gather | solution.py:19
  24.4 0.7 compare_select_fusion.4
  25.1 1.5 gather_fusion
  26.6 0.7 compare_and_fusion.2
  27.2 0.7 broadcast_select_fusion.1
  27.9 0.8 copy.48
  28.8 0.6 gather_fusion.1
  29.7 108.4 %all-gather.6.cloned.1.call-done = bf16[128,2,64,192]{3,2,1,0:T(8,128)(2,1)} async-done(((bf16[8,2,64,192]{3,2,1,0:T(8,128)(2,1)}), bf16[128,2,64,192]{3,2,1,0:T(8,128)(2,1)}) %all-gather.6.cloned.1.call-update) | async-done | bytes 6291472 | tf_op jit(solution)/shard_map/all_gather | solution.py:19
  138.1 8.3 %copy.50 = bf16[4,2,16,2,64,192]{5,4,3,2,1,0:T(8,128)(2,1)} copy(bf16[4,2,16,2,64,192]{5,4,3,1,0,2:T(8,128)(2,1)} %bitcast.37) | data formatting | bytes 12582912 | tf_op jit(solution)/shard_map/transpose | solution.py:23
  146.4 3.9 gather_fusion.2
  150.5 11.2 %all_to_all.15 = bf16[4,4,64,192]{3,2,1,0:T(8,128)(2,1)S(1)} all-to-all(bf16[4,4,64,192]{3,2,1,0:T(8,128)(2,1)S(1)} %broadcast_in_dim.45), channel_id=1, replica_groups=mesh['ka_0'=4,'ka_1'=2,'ka_2'=16,'col'=4] {'col'}, dimensions={0} | all-to-all | bytes 786432 | tf_op jit(solution)/shard_map/all_to_all | solution.py:32
  161.8 0.5 fusion
  162.3 192.0 %all-gather.4.cloned.1.call-done = bf16[2,2048,512]{2,1,0:T(8,128)(2,1)} async-done(((bf16[2,16,512]{2,1,0:T(8,128)(2,1)}), bf16[2,2048,512]{2,1,0:T(8,128)(2,1)}) %all-gather.4.cloned.1.call-update) | async-done | bytes 4194320 | tf_op jit(solution)/shard_map/all_gather | solution.py:71
  354.3 4.5 %convolution_convert_fusion = bf16[2,2048,384]{2,1,0:T(8,128)(2,1)S(1)} fusion(bf16[2,2048,512]{2,1,0:T(8,128)(2,1)} %all-gather.4.cloned.1.call-done, bf16[2,512,384]{1,2,0:T(8,128)(2,1)S(1)} %bitcast.43), kind=kOutput, calls=%fused_computation.3 | convolution fusion | flops 1612185600 | bytes 8126464 | tf_op jit(solution)/shard_map/qrm,qmx->qrx/dot_general | solution.py:69
  358.8 0.3 copy.67
  359.2 49.6 %all_to_all.16 = bf16[4,2,512,384]{3,2,1,0:T(8,128)(2,1)} all-to-all(bf16[4,2,512,384]{3,2,1,0:T(8,128)(2,1)S(1)} %bitcast.35), channel_id=1, replica_groups=mesh['ka_0'=4,'ka_1'=2,'ka_2'=16,'col'=4] {'col'}, dimensions={0} | all-to-all | bytes 6291456 | tf_op jit(solution)/shard_map/all_to_all | solution.py:49
  408.7 2.7 reduce_sum.32
  411.4 0.1 convert_reduce_fusion
  411.5 0.2 copy.57
  411.7 0.3 fusion.1
  412.0 0.1 copy.58
  412.2 8.4 %all_to_all.17 = bf16[4,2,64,192]{3,2,1,0:T(8,128)(2,1)S(1)} all-to-all(bf16[4,2,64,192]{3,2,1,0:T(8,128)(2,1)S(1)} %copy.59), channel_id=1, replica_groups=mesh['ka_0'=4,'ka_1'=2,'ka_2'=16,'col'=4] {'col'}, dimensions={0} | all-to-all | bytes 393216 | tf_op jit(solution)/shard_map/all_to_all | solution.py:49
  420.6 0.7 multiply_add_fusion
  (27 shorter events, 0.7 us)
Async XLA Ops:
  6.5 155.2 %copy-start = (bf16[2,512,256]{2,1,0:T(8,128)(2,1)S(1)}, bf16[2,512,256]{2,1,0:T(8,128)(2,1)}, u32[]{:S(2)}) copy-start(bf16[2,512,256]{2,1,0:T(8,128)(2,1)} %param.7) | copy-start | bytes 1572868
  6.5 131.6 %all-gather.6.cloned.1.call-start = ((), (), s32[]{:S(2)}) async-start(), calls=%async_computation.4 | async-start | bytes 8912896 | tf_op jit(solution)/shard_map/all_gather | solution.py:19
  24.3 329.9 %all-gather.4.cloned.1.call-start = ((), (), s32[]{:S(2)}) async-start(), calls=%async_computation.3 | async-start | bytes 4227072 | tf_op jit(solution)/shard_map/all_gather | solution.py:71
  408.7 11.9 %copy-start.1 = (bf16[2,64,192]{2,1,0:T(8,128)(2,1)S(1)}, bf16[2,64,192]{2,1,0:T(8,128)(2,1)}, u32[]{:S(2)}) copy-start(bf16[2,64,192]{2,1,0:T(8,128)(2,1)} %param.6) | copy-start | bytes 147460
  408.7 11.9 %copy-start.2 = (f32[2,64]{1,0:T(2,128)S(1)}, f32[2,64]{1,0:T(2,128)}, u32[]{:S(2)}) copy-start(f32[2,64]{1,0:T(2,128)} %param.9) | copy-start | bytes 1540
Sparse Core Ops, SparseCore 0:
  24.5 113.6 all-gather.5
  142.5 211.6 all-gather.3
where the time goes:
time: 429 us; the launch traced here: 428 us
  waiting for transfers between devices  300 us (70%)
  blocking collectives  87 us (20%)
  local copies, waits for them, and re-layouts  16.1 us (4%)
  between operations  13.6 us (3%)
  other arithmetic  5.77 us (1%)
  matrix products  5.3 us (1%)
    all_gather x1, waiting for transfers between devices, body(): lax.all_gather(slabs, KA, axis=1, tiled=True)  192 us
    all_gather x1, waiting for transfers between devices, gather_in_order(): pieces = lax.all_gather(pieces, axes[k], axis=0, tiled=True)  108 us
    all_to_all x2, blocking collectives, sent_and_summed(): lax.all_to_all(pieces, axis, split_axis=0, concat_axis=0, tiled=True)  58 us
    all_gather x2, blocking collectives, gather_in_order(): pieces = lax.all_gather(pieces, axes[k], axis=0, tiled=True)  17.8 us
    all_to_all x1, blocking collectives, sent_to_all(): lax.all_to_all(jnp.broadcast_to(array[None], (length, *array.shape)), axi...  11.2 us
  transfers between devices with their start and end apart: 2, of which 2 were waited for; matrix products, arithmetic and copies ran while one was open for 4% of the time, Pallas kernels for 0%

commit v1 on v0

--- a/solution.py
+++ b/solution.py
@@ -16,7 +16,9 @@
 def gather_in_order(array, axes, order):
     pieces = array[None]
     for k in order:
-        pieces = lax.all_gather(pieces, axes[k], axis=0, tiled=True)
+        pieces = jnp.concatenate(
+            lax.all_to_all(jnp.stack([pieces] * lax.axis_size(axes[k])), axes[k], 0, 0), axis=0
+        )
     carried = [lax.axis_size(axes[k]) for k in reversed(order)]
     pieces = pieces.reshape(*carried, *array.shape)
     turned = sorted(range(len(order)), key=lambda place: order[len(order) - 1 - place])

time: 429 us -> 523 us (1.22)
  waiting for transfers between devices: 300 us -> 382 us
  starting transfers between devices: 0.04 us -> 15.1 us
  blocking collectives: 87 us -> 80.6 us
    all_to_all x0 -> x1, waiting for transfers between devices: none -> 382 us  [gather_in_order(): lax.all_to_all(jnp.stack([pieces] * lax.axis_size(axes[k])), axes[k], 0, 0)]
    all_gather x1, waiting for transfers between devices: 192 us -> 0.02 us  [body(): lax.all_gather(slabs, KA, axis=1, tiled=True)]
    all_gather x1 -> x0, waiting for transfers between devices: 108 us -> none  [gather_in_order(): pieces = lax.all_gather(pieces, axes[k], axis=0, tiled=True)]
    all_to_all x0 -> x2, blocking collectives: none -> 20.4 us  [gather_in_order(): lax.all_to_all(jnp.stack([pieces] * lax.axis_size(axes[k])), axes[k], 0, 0)]
    all_gather x2 -> x0, blocking collectives: 17.8 us -> none  [gather_in_order(): pieces = lax.all_gather(pieces, axes[k], axis=0, tiled=True)]
    all_to_all x0 -> x1, starting transfers between devices: none -> 15.1 us  [gather_in_order(): lax.all_to_all(jnp.stack([pieces] * lax.axis_size(axes[k])), axes[k], 0, 0)]
    another operation x0 -> x3, local copies, waits for them, and re-layouts: none -> 12.6 us  [the longest x1 8.26 us: gather_in_order(): pieces = pieces.reshape(*carried, *array.shape)]
    all_to_all x2, blocking collectives: 58 us -> 48.6 us  [sent_and_summed(): lax.all_to_all(pieces, axis, split_axis=0, concat_axis=0, tiled=True)]
  transfers between devices with their start and end apart: 2 -> 2, of which waited for: 2 -> 1; matrix products, arithmetic and copies ran while one was open for 4% -> 3% of each run, Pallas kernels for 0% -> 0%
where the time goes in v1:
time: 523 us; the launch traced here: 522 us
  waiting for transfers between devices  382 us (73%)
  blocking collectives  80.6 us (15%)
  local copies, waits for them, and re-layouts  19.8 us (4%)
  starting transfers between devices  15.1 us (3%)
  between operations  13.6 us (3%)
  other arithmetic  5.41 us (1%)
  matrix products  5.3 us (1%)
    all_to_all x1, waiting for transfers between devices, gather_in_order(): lax.all_to_all(jnp.stack([pieces] * lax.axis_size(axes[k])), axes[k], 0, 0)  382 us
    all_to_all x2, blocking collectives, sent_and_summed(): lax.all_to_all(pieces, axis, split_axis=0, concat_axis=0, tiled=True)  48.6 us
    all_to_all x2, blocking collectives, gather_in_order(): lax.all_to_all(jnp.stack([pieces] * lax.axis_size(axes[k])), axes[k], 0, 0)  20.4 us
    all_to_all x1, starting transfers between devices, gather_in_order(): lax.all_to_all(jnp.stack([pieces] * lax.axis_size(axes[k])), axes[k], 0, 0)  15.1 us
    all_to_all x1, blocking collectives, sent_to_all(): lax.all_to_all(jnp.broadcast_to(array[None], (length, *array.shape)), axi...  11.6 us
  transfers between devices with their start and end apart: 2, of which 1 were waited for; matrix products, arithmetic and copies ran while one was open for 3% of the time, Pallas kernels for 0%

profile of v1, /device:TPU:1, one launch (start us, length us, event | category | flops | bytes accessed | tf_op | source)
XLA Modules:
  0.0 522.1 jit_solution(14933848081847449666)
XLA Ops:
  6.5 1.0 pad_maximum_fusion
  7.5 9.5 %all_to_all.30 = bf16[2,1,2,64,192]{4,3,2,1,0:T(8,128)(2,1)S(1)} all-to-all(bf16[2,1,2,64,192]{4,3,2,1,0:T(8,128)(2,1)S(1)} %pad_maximum_fusion), channel_id=1, replica_groups=mesh['ka_0'=4,'ka_1'=2,'ka_2'=16,'col'=4] {'ka_1'}, dimensions={0} | all-to-all | bytes 196608 | tf_op jit(solution)/shard_map/all_to_all | solution.py:20
  17.0 10.9 %all_to_all.31 = bf16[4,2,2,64,192]{4,3,2,1,0:T(8,128)(2,1)S(1)} all-to-all(bf16[4,2,2,64,192]{4,3,2,1,0:T(8,128)(2,1)S(1)} %stack.10), channel_id=1, replica_groups=mesh['ka_0'=4,'ka_1'=2,'ka_2'=16,'col'=4] {'ka_0'}, dimensions={0} | all-to-all | bytes 786432 | tf_op jit(solution)/shard_map/all_to_all | solution.py:20
  27.9 4.3 stack.11
  32.2 15.1 %all-to-all-start.2 = ((bf16[16,8,2,64,192]{4,3,2,1,0:T(8,128)(2,1)}), bf16[16,8,2,64,192]{4,3,2,1,0:T(8,128)(2,1)}, u32[]{:S(2)}, u32[]{:S(2)}) async-start(bf16[16,8,2,64,192]{4,3,2,1,0:T(8,128)(2,1)} %stack.11), calls=%async_computation.2 | async-start | bytes 16777216 | tf_op jit(solution)/shard_map/all_to_all | solution.py:20
  47.4 1.5 gather_fusion
  48.9 0.7 broadcast_select_fusion.1
  49.7 0.1 copy.40
  49.8 0.6 gather_fusion.1
  50.8 382.2 %all-to-all-done.2 = bf16[16,8,2,64,192]{4,3,2,1,0:T(8,128)(2,1)} async-done(((bf16[16,8,2,64,192]{4,3,2,1,0:T(8,128)(2,1)}), bf16[16,8,2,64,192]{4,3,2,1,0:T(8,128)(2,1)}, u32[]{:S(2)}, u32[]{:S(2)}) %all-to-all-start.2) | async-done | bytes 6291488 | tf_op jit(solution)/shard_map/all_to_all | solution.py:20
  433.0 8.3 %copy.42 = bf16[16,4,2,2,64,192]{5,4,3,0,2,1:T(8,128)(2,1)} copy(bf16[16,4,2,2,64,192]{5,4,3,2,1,0:T(8,128)(2,1)} %bitcast.5) | data formatting | bytes 12582912 | tf_op jit(solution)/shard_map/reshape;reshape | solution.py:23
  441.2 3.9 gather_fusion.2
  445.3 11.6 %all_to_all.32 = bf16[4,4,64,192]{3,2,1,0:T(8,128)(2,1)S(1)} all-to-all(bf16[4,4,64,192]{3,2,1,0:T(8,128)(2,1)S(1)} %broadcast_in_dim.41), channel_id=1, replica_groups=mesh['ka_0'=4,'ka_1'=2,'ka_2'=16,'col'=4] {'col'}, dimensions={0} | all-to-all | bytes 786432 | tf_op jit(solution)/shard_map/all_to_all | solution.py:34
  456.9 0.5 fusion
  457.5 4.5 convolution_convert_fusion
  462.1 0.3 copy.59
  462.4 40.2 %all_to_all.33 = bf16[4,2,512,384]{3,2,1,0:T(8,128)(2,1)} all-to-all(bf16[4,2,512,384]{3,2,1,0:T(8,128)(2,1)S(1)} %bitcast.37), channel_id=1, replica_groups=mesh['ka_0'=4,'ka_1'=2,'ka_2'=16,'col'=4] {'col'}, dimensions={0} | all-to-all | bytes 6291456 | tf_op jit(solution)/shard_map/all_to_all | solution.py:51
  502.6 2.7 reduce_sum.32
  505.3 0.1 convert_reduce_fusion
  505.4 0.2 copy.49
  505.6 0.3 fusion.1
  505.9 0.1 copy.50
  506.0 8.4 %all_to_all.34 = bf16[4,2,64,192]{3,2,1,0:T(8,128)(2,1)S(1)} all-to-all(bf16[4,2,64,192]{3,2,1,0:T(8,128)(2,1)S(1)} %copy.51), channel_id=1, replica_groups=mesh['ka_0'=4,'ka_1'=2,'ka_2'=16,'col'=4] {'col'}, dimensions={0} | all-to-all | bytes 393216 | tf_op jit(solution)/shard_map/all_to_all | solution.py:51
  514.5 0.7 multiply_add_fusion
  (33 shorter events, 0.8 us)
Async XLA Ops:
  6.5 450.4 %copy-start = (bf16[2,512,256]{2,1,0:T(8,128)(2,1)S(1)}, bf16[2,512,256]{2,1,0:T(8,128)(2,1)}, u32[]{:S(2)}) copy-start(bf16[2,512,256]{2,1,0:T(8,128)(2,1)} %param.7) | copy-start | bytes 1572868
  32.2 15.2 %copy-start.4 = (s32[2]{0:T(128)S(1)}, s32[2]{0:T(128)}, u32[]{:S(2)}) copy-start(s32[2]{0:T(128)} %param.10) | copy-start | bytes 28
  32.2 17.4 %copy-start.2 = (s32[2,256]{1,0:T(2,128)S(1)}, s32[2,256]{1,0:T(2,128)}, u32[]{:S(2)}) copy-start(s32[2,256]{1,0:T(2,128)} %param.11) | copy-start | bytes 6148
  32.2 400.7 %all-to-all-start.2 = ((bf16[16,8,2,64,192]{4,3,2,1,0:T(8,128)(2,1)}), bf16[16,8,2,64,192]{4,3,2,1,0:T(8,128)(2,1)}, u32[]{:S(2)}, u32[]{:S(2)}) async-start(bf16[16,8,2,64,192]{4,3,2,1,0:T(8,128)(2,1)} %stack.11), calls=%async_computation.2 | async-start | bytes 16777216 | tf_op jit(solution)/shard_map/all_to_all | solution.py:20
  47.3 410.2 %all-gather.2.cloned.1.call-start = ((), (), s32[]{:S(2)}) async-start(), calls=%async_computation.6 | async-start | bytes 4227072 | tf_op jit(solution)/shard_map/all_gather | solution.py:73
  502.6 11.9 %copy-start.1 = (bf16[2,64,192]{2,1,0:T(8,128)(2,1)S(1)}, bf16[2,64,192]{2,1,0:T(8,128)(2,1)}, u32[]{:S(2)}) copy-start(bf16[2,64,192]{2,1,0:T(8,128)(2,1)} %param.6) | copy-start | bytes 147460
  502.6 11.9 %copy-start.3 = (f32[2,64]{1,0:T(2,128)S(1)}, f32[2,64]{1,0:T(2,128)}, u32[]{:S(2)}) copy-start(f32[2,64]{1,0:T(2,128)} %param.9) | copy-start | bytes 1540
Sparse Core Ops, SparseCore 0:
  52.5 363.6 all-gather.1
